TPU v7x, 32 devices: a whole 2x2x4 slice. The times are simulated.
32 devices in a mesh: blk: 8 (over y, x, core), rep: 4 (over z).
Axes of the slice: x: 2, y: 2, z: 4, core: 2. Of those that a mesh axis runs over, the one named last changes fastest.
Arguments:
- image: bfloat16 [4096, 1024], P(('blk', 'rep')), may hold values from -100 to 100
- text: bfloat16 [4096, 1024], P(('blk', 'rep')), may hold values from -100 to 100
- positive: int32 [8, 512], P('blk', 'rep'), may hold values from 0 to 511, each once within a row
- logit_scale: float32 [1], replicated, may hold values from 85 to 270
Outputs:
- row_loss: float32 [4096], P(('blk', 'rep'))
- col_loss: float32 [4096], P(('blk', 'rep'))
- img_grad: float32 [4096, 1024], P(('blk', 'rep'))
- txt_grad: float32 [4096, 1024], P(('blk', 'rep'))
Inputs may be any that keep to these rules, and one draw needn't show every extreme that they name: Each row of positive names every index of its block once.
All inputs are finite; a program needn't handle non-finite values.
Results may differ from a plain program's by a relative error of at most 0.0081.
The roundings to bfloat16 on the way count: a program that leaves them out, or rounds other values in their place, can miss the bound.
Values may be sent and summed in bfloat16 or wider, within the bound.
No kernel may reach another device: no remote copies, remote signals or barrier semaphores. Data moves between devices by JAX's collectives and lax.ppermute only.
A program may use at most 64 MiB of HBM per device.

v0:
```python
import jax
import jax.numpy as jnp
from jax import lax
from jax.sharding import PartitionSpec as P

STEPS = 4


def passed_along(array, axis, by):
    count = lax.axis_size(axis)
    return lax.ppermute(array, axis, [(i, (i + by) % count) for i in range(count)])


def combined_all(part, axis, combine):
    gathered = jax.tree.map(lambda a: lax.all_gather(a, axis), part)

    def take(source):
        return jax.tree.map(lambda a: lax.dynamic_index_in_dim(a, source, 0, False), gathered)

    return lax.fori_loop(
        1, lax.axis_size(axis), lambda source, state: combine(state, take(source)), take(0)
    )


def normalize(values):
    widened = values.astype(jnp.float32)
    inverse = lax.rsqrt(jnp.sum(widened * widened, axis=-1, keepdims=True) + 1e-06)
    return (widened * inverse, inverse)


def combine_stats(earlier, later):
    highest = jnp.maximum(earlier[0], later[0])
    summed = earlier[1] * jnp.exp(earlier[0] - highest) + later[1] * jnp.exp(later[0] - highest)
    return (highest, summed, earlier[2] + later[2])


def tile_scores(img_part, text_tile, factor):
    return factor * jnp.einsum("id,jd->ij", img_part, text_tile, preferred_element_type=jnp.float32)


def tile_weights(img_part, text_tile, factor, row_lse, col_lse, onehot):
    scores = tile_scores(img_part, text_tile, factor)
    weight = 0.5 * (jnp.exp(scores - row_lse[:, None]) + jnp.exp(scores - col_lse[None, :]))
    if onehot is not None:
        weight = weight - onehot
    return weight.astype(jnp.bfloat16)


def on_device(image, text, positive, logit_scale):
    factor = logit_scale[0]
    row_count = image.shape[0]
    width = image.shape[1]
    quarter = lax.axis_index("rep")
    img_unit, img_inverse = normalize(image)
    txt_unit, txt_inverse = normalize(text)
    img_tile = img_unit.astype(jnp.bfloat16)
    txt_own = txt_unit.astype(jnp.bfloat16)
    home_tile = lax.all_gather(txt_own, "rep", axis=0, tiled=True)
    block_rows = home_tile.shape[0]
    columns = lax.broadcasted_iota(jnp.int32, (row_count, block_rows), 1)
    onehot = (positive[0][:, None] == columns).astype(jnp.float32)
    kept = []
    moving = img_tile
    for loop_step in range(STEPS):
        if loop_step > 0:
            moving = passed_along(moving, "blk", -1)
            row_max, row_sum = passed_along((row_max, row_sum), "blk", -1)
        kept.append(moving)
        scores = tile_scores(moving, home_tile, factor)
        row_peak = jnp.max(scores, axis=1)
        col_peak = jnp.max(scores, axis=0)
        col_part = jnp.sum(jnp.exp(scores - col_peak[None, :]), axis=0)
        if loop_step == 0:
            row_max = row_peak
            row_sum = jnp.sum(jnp.exp(scores - row_peak[:, None]), axis=1)
            row_pos = jnp.sum(onehot * scores, axis=1)
            col_max, col_sum, col_pos = (col_peak, col_part, jnp.sum(onehot * scores, axis=0))
        else:
            highest = jnp.maximum(row_max, row_peak)
            row_sum = row_sum * jnp.exp(row_max - highest) + jnp.sum(
                jnp.exp(scores - highest[:, None]), axis=1
            )
            row_max = highest
            col_max, col_sum, col_pos = combine_stats(
                (col_max, col_sum, col_pos), (col_peak, col_part, jnp.zeros_like(col_peak))
            )
    col_max, col_sum, col_pos = combined_all((col_max, col_sum, col_pos), "rep", combine_stats)
    col_lse = col_max + jnp.log(col_sum)
    row_lse = row_max + jnp.log(row_sum)
    travel = (row_lse, jnp.zeros((row_count, width), jnp.float32))
    text_terms = jnp.zeros((block_rows, width), jnp.float32)
    for loop_step in range(STEPS - 1, -1, -1):
        if loop_step < STEPS - 1:
            travel = passed_along((travel[0], travel[1]), "blk", 1)
        tile = kept[loop_step]
        weight = tile_weights(
            tile, home_tile, factor, travel[0], col_lse, onehot if loop_step == 0 else None
        )
        travel = (
            travel[0],
            travel[1] + jnp.dot(weight, home_tile, preferred_element_type=jnp.float32),
        )
        text_terms = text_terms + jnp.einsum(
            "ij,id->jd", weight, tile, preferred_element_type=jnp.float32
        )
    row_lse, img_acc = travel
    col_lse_home, col_pos_home = (col_lse, col_pos)
    row_loss = row_lse - row_pos
    text_share = lax.psum_scatter(text_terms, "rep", scatter_dimension=0, tiled=True)
    img_sum = factor * img_acc
    txt_sum = factor * text_share
    img_grad = (
        img_sum - img_unit * jnp.sum(img_unit * img_sum, axis=-1, keepdims=True)
    ) * img_inverse
    txt_grad = (
        txt_sum - txt_unit * jnp.sum(txt_unit * txt_sum, axis=-1, keepdims=True)
    ) * txt_inverse
    col_whole = col_lse_home - col_pos_home
    col_loss = lax.dynamic_slice_in_dim(col_whole, quarter * row_count, row_count)
    return (row_loss, col_loss, img_grad, txt_grad)


def solution(mesh):
    placed = (P(("blk", "rep"), None), P(("blk", "rep"), None), P("blk", "rep"), P())
    return jax.shard_map(
        on_device,
        mesh=mesh,
        in_specs=placed,
        out_specs=(
            P(("blk", "rep")),
            P(("blk", "rep")),
            P(("blk", "rep"), None),
            P(("blk", "rep"), None),
        ),
        check_vma=False,
    )
```

profile of v0, /device:TPU:0, one launch (start us, length us, event | category | flops | bytes accessed | tf_op | source)
XLA Modules:
  0.0 154.7 jit_solution(10748212426085432188)
XLA Ops:
  7.2 1.1 fusion.13
  8.3 1.8 %fusion.2 = bf16[128,1024]{1,0:T(8,128)(2,1)} fusion(bf16[128,1024]{1,0:T(8,128)(2,1)} %param.7, f32[128]{0:T(128)S(1)} %add_rsqrt_fusion), kind=kLoop, calls=%fused_computation.14 | loop fusion | flops 393216 | bytes 524800 | tf_op jit(solution)/shard_map/convert_element_type | solution.py:57
  10.2 1.1 fusion.9
  11.2 1.1 fusion.5
  12.3 3.4 %collective-permute-start.1 = (bf16[128,1024]{1,0:T(8,128)(2,1)S(1)}, bf16[128,1024]{1,0:T(8,128)(2,1)S(1)}, u32[]{:S(2)}, u32[]{:S(2)}) collective-permute-start(bf16[128,1024]{1,0:T(8,128)(2,1)S(1)} %fusion.5), channel_id=1, source_target_pairs={{0,28},{4,0},{8,4},{12,8},{16,12},{20,16},{24,20},{28,24},{1,29},{... | collective-permute-start | bytes 786440 | tf_op jit(solution)/shard_map/ppermute | solution.py:11
  15.7 3.9 %collective-permute-done.1 = bf16[128,1024]{1,0:T(8,128)(2,1)S(1)} collective-permute-done((bf16[128,1024]{1,0:T(8,128)(2,1)S(1)}, bf16[128,1024]{1,0:T(8,128)(2,1)S(1)}, u32[]{:S(2)}, u32[]{:S(2)}) %collective-permute-start.1) | collective-permute-done | bytes 262176 | tf_op jit(solution)/shard_map/ppermute | solution.py:11
  19.6 2.8 %collective-permute-start.3 = (bf16[128,1024]{1,0:T(8,128)(2,1)S(1)}, bf16[128,1024]{1,0:T(8,128)(2,1)S(1)}, u32[]{:S(2)}, u32[]{:S(2)}) collective-permute-start(bf16[128,1024]{1,0:T(8,128)(2,1)S(1)} %collective-permute-done.1), channel_id=1, source_target_pairs={{0,28},{4,0},{8,4},{12,8},{16,12},{20,16},{24,20},{28,24},{1,29},{... | collective-permute-start | bytes 786440 | tf_op jit(solution)/shard_map/ppermute | solution.py:11
  23.1 3.2 %collective-permute-done.3 = bf16[128,1024]{1,0:T(8,128)(2,1)S(1)} collective-permute-done((bf16[128,1024]{1,0:T(8,128)(2,1)S(1)}, bf16[128,1024]{1,0:T(8,128)(2,1)S(1)}, u32[]{:S(2)}, u32[]{:S(2)}) %collective-permute-start.3) | collective-permute-done | bytes 262176 | tf_op jit(solution)/shard_map/ppermute | solution.py:11
  26.3 3.2 %collective-permute-start.5 = (bf16[128,1024]{1,0:T(8,128)(2,1)S(1)}, bf16[128,1024]{1,0:T(8,128)(2,1)S(1)}, u32[]{:S(2)}, u32[]{:S(2)}) collective-permute-start(bf16[128,1024]{1,0:T(8,128)(2,1)S(1)} %collective-permute-done.3), channel_id=1, source_target_pairs={{0,28},{4,0},{8,4},{12,8},{16,12},{20,16},{24,20},{28,24},{1,29},{... | collective-permute-start | bytes 786440 | tf_op jit(solution)/shard_map/ppermute | solution.py:11
  29.5 11.4 %all-gather.6.cloned.1.call-done = bf16[512,1024]{1,0:T(8,128)(2,1)} async-done(((bf16[128,1024]{1,0:T(8,128)(2,1)}), bf16[512,1024]{1,0:T(8,128)(2,1)}) %all-gather.6.cloned.1.call-update) | async-done | bytes 1048592 | tf_op jit(solution)/shard_map/all_gather | solution.py:58
  41.0 1.9 %fusion.25 = (f32[512]{0:T(512)S(1)}, f32[128]{0:T(128)S(1)}, f32[128,512]{1,0:T(8,128)S(1)}) fusion(bf16[128,1024]{1,0:T(8,128)(2,1)S(1)} %fusion.5, bf16[512,1024]{1,0:T(8,128)(2,1)} %all-gather.6.cloned.1.call-done, f32[]{:T(128)} %bitcast.52), kind=kOutput, calls=%fused_computation.64 | convolution fusion | flops 134413696 | bytes 1575428 | tf_op jit(solution)/shard_map/id,jd->ij/dot_general | solution.py:38
  43.1 11.9 %all-gather.3 = f32[4,1,512]{2,1,0:T(1,128)S(1)} all-gather(f32[1,1,512]{2,1,0:T(1,128)S(1)} %bitcast.77), channel_id=2, replica_groups=mesh['blk'=8,'rep'=4] {'rep'}, dimensions={0}, use_global_device_ids=true | all-gather | bytes 10240 | tf_op jit(solution)/shard_map/all_gather | solution.py:15
  55.1 2.5 %collective-permute-start.6 = (f32[128]{0:T(128)S(1)}, f32[128]{0:T(128)S(1)}, u32[]{:S(2)}, u32[]{:S(2)}) collective-permute-start(f32[128]{0:T(128)S(1)} %get-tuple-element.188), channel_id=1, source_target_pairs={{0,28},{4,0},{8,4},{12,8},{16,12},{20,16},{24,20},{28,24},{1,29},{... | collective-permute-start | bytes 1544 | tf_op jit(solution)/shard_map/ppermute | solution.py:11
  58.7 0.6 fusion.27
  59.6 1.8 %collective-permute-start.7 = (f32[128]{0:T(128)S(1)}, f32[128]{0:T(128)S(1)}, u32[]{:S(2)}, u32[]{:S(2)}) collective-permute-start(f32[128]{0:T(128)S(1)} %multiply_add_fusion.2), channel_id=1, source_target_pairs={{0,28},{4,0},{8,4},{12,8},{16,12},{20,16},{24,20},{28,24},{1,29},{... | collective-permute-start | bytes 1544 | tf_op jit(solution)/shard_map/ppermute | solution.py:11
  61.5 1.8 %collective-permute-start.4 = (f32[128]{0:T(128)S(1)}, f32[128]{0:T(128)S(1)}, u32[]{:S(2)}, u32[]{:S(2)}) collective-permute-start(f32[128]{0:T(128)S(1)} %max.62), channel_id=1, source_target_pairs={{0,28},{4,0},{8,4},{12,8},{16,12},{20,16},{24,20},{28,24},{1,29},{... | collective-permute-start | bytes 1544 | tf_op jit(solution)/shard_map/ppermute | solution.py:11
  63.5 1.8 %collective-permute-start.8 = (f32[128]{0:T(128)S(1)}, f32[128]{0:T(128)S(1)}, u32[]{:S(2)}, u32[]{:S(2)}) collective-permute-start(f32[128]{0:T(128)S(1)} %multiply_add_fusion.1), channel_id=1, source_target_pairs={{0,28},{4,0},{8,4},{12,8},{16,12},{20,16},{24,20},{28,24},{1,29},{... | collective-permute-start | bytes 1544 | tf_op jit(solution)/shard_map/ppermute | solution.py:11
  65.6 11.9 %all-gather.2 = f32[4,1,512]{2,1,0:T(1,128)S(1)} all-gather(f32[1,1,512]{2,1,0:T(1,128)S(1)} %get-tuple-element.223), channel_id=1, replica_groups=mesh['blk'=8,'rep'=4] {'rep'}, dimensions={0}, use_global_device_ids=true | all-gather | bytes 10240 | tf_op jit(solution)/shard_map/all_gather | solution.py:15
  77.6 11.9 %all-gather.1 = f32[4,1,512]{2,1,0:T(1,128)S(1)} all-gather(f32[1,1,512]{2,1,0:T(1,128)S(1)} %get-tuple-element.224), channel_id=1, replica_groups=mesh['blk'=8,'rep'=4] {'rep'}, dimensions={0}, use_global_device_ids=true | all-gather | bytes 10240 | tf_op jit(solution)/shard_map/all_gather | solution.py:15
  89.9 3.9 %collective-permute-done.9 = f32[128]{0:T(128)S(1)} collective-permute-done((f32[128]{0:T(128)S(1)}, f32[128]{0:T(128)S(1)}, u32[]{:S(2)}, u32[]{:S(2)}) %collective-permute-start.9) | collective-permute-done | bytes 544 | tf_op jit(solution)/shard_map/ppermute | solution.py:11
  94.3 3.4 %collective-permute-done.10 = f32[128]{0:T(128)S(1)} collective-permute-done((f32[128]{0:T(128)S(1)}, f32[128]{0:T(128)S(1)}, u32[]{:S(2)}, u32[]{:S(2)}) %collective-permute-start.10) | collective-permute-done | bytes 544 | tf_op jit(solution)/shard_map/ppermute | solution.py:11
  98.2 3.3 %collective-permute-done.11 = f32[128]{0:T(128)S(1)} collective-permute-done((f32[128]{0:T(128)S(1)}, f32[128]{0:T(128)S(1)}, u32[]{:S(2)}, u32[]{:S(2)}) %collective-permute-start.11) | collective-permute-done | bytes 544 | tf_op jit(solution)/shard_map/ppermute | solution.py:11
  101.5 0.6 fusion.22
  102.1 1.9 %add_add_fusion = f32[512,1024]{1,0:T(8,128)} fusion(f32[512,1024]{1,0:T(8,128)S(1)} %fusion.22, f32[512,1024]{1,0:T(8,128)S(1)} %fusion.19, f32[512,1024]{1,0:T(8,128)S(1)} %fusion.18, bf16[128,1024]{1,0:T(8,128)(2,1)S(1)} %collective-permute-done.5, f32[128,512]{1,0:T(8,128)S(1)} %get-tuple-element.228, f32[512]{0:T(512)S(1)} %get-tuple-element.220, ...), kind=kOutput, calls=%fused_computation.4 | convolution fusion | flops 136118272 | bytes 8915456 | tf_op jit(solution)/shard_map/ij,id->jd/dot_general | solution.py:103
  104.5 9.5 %collective-permute-done.12 = f32[128,1024]{1,0:T(8,128)S(1)} collective-permute-done((f32[128,1024]{1,0:T(8,128)S(1)}, f32[128,1024]{1,0:T(8,128)S(1)}, u32[]{:S(2)}, u32[]{:S(2)}) %collective-permute-start.12) | collective-permute-done | bytes 524320 | tf_op jit(solution)/shard_map/ppermute | solution.py:11
  114.4 9.5 %collective-permute-done.13 = f32[128,1024]{1,0:T(8,128)S(1)} collective-permute-done((f32[128,1024]{1,0:T(8,128)S(1)}, f32[128,1024]{1,0:T(8,128)S(1)}, u32[]{:S(2)}, u32[]{:S(2)}) %collective-permute-start.13) | collective-permute-done | bytes 524320 | tf_op jit(solution)/shard_map/ppermute | solution.py:11
  124.4 0.6 dynamic_slice.46
  125.5 8.4 %collective-permute-done.14 = f32[128,1024]{1,0:T(8,128)S(1)} collective-permute-done((f32[128,1024]{1,0:T(8,128)S(1)}, f32[128,1024]{1,0:T(8,128)S(1)}, u32[]{:S(2)}, u32[]{:S(2)}) %collective-permute-start.14) | collective-permute-done | bytes 524320 | tf_op jit(solution)/shard_map/ppermute | solution.py:11
  134.3 1.0 fusion.8
  135.4 9.2 %reduce-scatter.2.cloned.1.call-done = f32[128,1024]{1,0:T(8,128)} async-done(((f32[512,1024]{1,0:T(8,128)}), f32[128,1024]{1,0:T(8,128)}) %reduce-scatter.2.cloned.1.call-update) | async-done | bytes 524304 | tf_op jit(solution)/shard_map/reduce_scatter | solution.py:109
  144.5 1.3 fusion.10
  145.8 2.1 %fusion.12 = f32[128,1024]{1,0:T(8,128)} fusion(bf16[128,1024]{1,0:T(8,128)(2,1)S(1)} %copy-done.1, f32[128,1024]{1,0:T(8,128)} %reduce-scatter.2.cloned.1.call-done, f32[128]{0:T(128)S(1)} %fusion.10, f32[]{:T(128)} %bitcast.54, f32[128]{0:T(128)S(1)} %add_rsqrt_fusion), kind=kLoop, calls=%fused_computation.26 | loop fusion | flops 786432 | bytes 1311748 | tf_op jit(solution)/shard_map/mul | solution.py:115
  (69 shorter events, 6.2 us)
Async XLA Ops:
  7.2 35.7 %copy-start.3 = (s32[1,128]{1,0:T(1,128)S(1)}, s32[1,128]{1,0:T(1,128)}, u32[]{:S(2)}) copy-start(s32[1,128]{1,0:T(1,128)} %param.8) | copy-start | bytes 1540
  7.2 33.8 %all-gather.6.cloned.1.call-start = ((), (), s32[]{:S(2)}) async-start(), calls=%async_computation.1 | async-start | bytes 1310720 | tf_op jit(solution)/shard_map/all_gather | solution.py:58
  10.1 134.4 %reduce-scatter.2.cloned.1.call-start = ((), (), s32[]{:S(2)}) async-start(), calls=%async_computation.2 | async-start | bytes 2621440 | tf_op jit(solution)/shard_map/reduce_scatter | solution.py:109
  12.3 7.3 %collective-permute-start.1 = (bf16[128,1024]{1,0:T(8,128)(2,1)S(1)}, bf16[128,1024]{1,0:T(8,128)(2,1)S(1)}, u32[]{:S(2)}, u32[]{:S(2)}) collective-permute-start(bf16[128,1024]{1,0:T(8,128)(2,1)S(1)} %fusion.5), channel_id=1, source_target_pairs={{0,28},{4,0},{8,4},{12,8},{16,12},{20,16},{24,20},{28,24},{1,29},{... | collective-permute-start | bytes 786440 | tf_op jit(solution)/shard_map/ppermute | solution.py:11
  19.6 6.7 %collective-permute-start.3 = (bf16[128,1024]{1,0:T(8,128)(2,1)S(1)}, bf16[128,1024]{1,0:T(8,128)(2,1)S(1)}, u32[]{:S(2)}, u32[]{:S(2)}) collective-permute-start(bf16[128,1024]{1,0:T(8,128)(2,1)S(1)} %collective-permute-done.1), channel_id=1, source_target_pairs={{0,28},{4,0},{8,4},{12,8},{16,12},{20,16},{24,20},{28,24},{1,29},{... | collective-permute-start | bytes 786440 | tf_op jit(solution)/shard_map/ppermute | solution.py:11
  26.3 32.4 %collective-permute-start.5 = (bf16[128,1024]{1,0:T(8,128)(2,1)S(1)}, bf16[128,1024]{1,0:T(8,128)(2,1)S(1)}, u32[]{:S(2)}, u32[]{:S(2)}) collective-permute-start(bf16[128,1024]{1,0:T(8,128)(2,1)S(1)} %collective-permute-done.3), channel_id=1, source_target_pairs={{0,28},{4,0},{8,4},{12,8},{16,12},{20,16},{24,20},{28,24},{1,29},{... | collective-permute-start | bytes 786440 | tf_op jit(solution)/shard_map/ppermute | solution.py:11
  41.0 16.6 %copy-start = (bf16[512,1024]{1,0:T(8,128)(2,1)S(1)}, bf16[512,1024]{1,0:T(8,128)(2,1)}, u32[]{:S(2)}) copy-start(bf16[512,1024]{1,0:T(8,128)(2,1)} %all-gather.6.cloned.1.call-done) | copy-start | bytes 3145732
  55.0 4.3 %collective-permute-start = (f32[128]{0:T(128)S(1)}, f32[128]{0:T(128)S(1)}, u32[]{:S(2)}, u32[]{:S(2)}) collective-permute-start(f32[128]{0:T(128)S(1)} %get-tuple-element.198), channel_id=1, source_target_pairs={{0,28},{4,0},{8,4},{12,8},{16,12},{20,16},{24,20},{28,24},{1,29},{... | collective-permute-start | bytes 1544 | tf_op jit(solution)/shard_map/ppermute | solution.py:11
  55.1 4.5 %collective-permute-start.6 = (f32[128]{0:T(128)S(1)}, f32[128]{0:T(128)S(1)}, u32[]{:S(2)}, u32[]{:S(2)}) collective-permute-start(f32[128]{0:T(128)S(1)} %get-tuple-element.188), channel_id=1, source_target_pairs={{0,28},{4,0},{8,4},{12,8},{16,12},{20,16},{24,20},{28,24},{1,29},{... | collective-permute-start | bytes 1544 | tf_op jit(solution)/shard_map/ppermute | solution.py:11
  59.3 2.2 %collective-permute-start.2 = (f32[128]{0:T(128)S(1)}, f32[128]{0:T(128)S(1)}, u32[]{:S(2)}, u32[]{:S(2)}) collective-permute-start(f32[128]{0:T(128)S(1)} %max.61), channel_id=1, source_target_pairs={{0,28},{4,0},{8,4},{12,8},{16,12},{20,16},{24,20},{28,24},{1,29},{... | collective-permute-start | bytes 1544 | tf_op jit(solution)/shard_map/ppermute | solution.py:11
  59.6 3.9 %collective-permute-start.7 = (f32[128]{0:T(128)S(1)}, f32[128]{0:T(128)S(1)}, u32[]{:S(2)}, u32[]{:S(2)}) collective-permute-start(f32[128]{0:T(128)S(1)} %multiply_add_fusion.2), channel_id=1, source_target_pairs={{0,28},{4,0},{8,4},{12,8},{16,12},{20,16},{24,20},{28,24},{1,29},{... | collective-permute-start | bytes 1544 | tf_op jit(solution)/shard_map/ppermute | solution.py:11
  61.5 3.9 %collective-permute-start.4 = (f32[128]{0:T(128)S(1)}, f32[128]{0:T(128)S(1)}, u32[]{:S(2)}, u32[]{:S(2)}) collective-permute-start(f32[128]{0:T(128)S(1)} %max.62), channel_id=1, source_target_pairs={{0,28},{4,0},{8,4},{12,8},{16,12},{20,16},{24,20},{28,24},{1,29},{... | collective-permute-start | bytes 1544 | tf_op jit(solution)/shard_map/ppermute | solution.py:11
  63.5 26.2 %collective-permute-start.8 = (f32[128]{0:T(128)S(1)}, f32[128]{0:T(128)S(1)}, u32[]{:S(2)}, u32[]{:S(2)}) collective-permute-start(f32[128]{0:T(128)S(1)} %multiply_add_fusion.1), channel_id=1, source_target_pairs={{0,28},{4,0},{8,4},{12,8},{16,12},{20,16},{24,20},{28,24},{1,29},{... | collective-permute-start | bytes 1544 | tf_op jit(solution)/shard_map/ppermute | solution.py:11
  89.8 3.9 %collective-permute-start.9 = (f32[128]{0:T(128)S(1)}, f32[128]{0:T(128)S(1)}, u32[]{:S(2)}, u32[]{:S(2)}) collective-permute-start(f32[128]{0:T(128)S(1)} %log_add_fusion.1), channel_id=1, source_target_pairs={{0,4},{4,8},{8,12},{12,16},{16,20},{20,24},{24,28},{28,0},{1,5},{5... | collective-permute-start | bytes 1544 | tf_op jit(solution)/shard_map/ppermute | solution.py:11
  93.7 3.9 %collective-permute-start.10 = (f32[128]{0:T(128)S(1)}, f32[128]{0:T(128)S(1)}, u32[]{:S(2)}, u32[]{:S(2)}) collective-permute-start(f32[128]{0:T(128)S(1)} %collective-permute-done.9), channel_id=1, source_target_pairs={{0,4},{4,8},{8,12},{12,16},{16,20},{20,24},{24,28},{28,0},{1,5},{5... | collective-permute-start | bytes 1544 | tf_op jit(solution)/shard_map/ppermute | solution.py:11
  97.6 3.9 %collective-permute-start.11 = (f32[128]{0:T(128)S(1)}, f32[128]{0:T(128)S(1)}, u32[]{:S(2)}, u32[]{:S(2)}) collective-permute-start(f32[128]{0:T(128)S(1)} %collective-permute-done.10), channel_id=1, source_target_pairs={{0,4},{4,8},{8,12},{12,16},{16,20},{20,24},{24,28},{28,0},{1,5},{5... | collective-permute-start | bytes 1544 | tf_op jit(solution)/shard_map/ppermute | solution.py:11
  104.4 29.4 %copy-start.2 = (bf16[128,1024]{1,0:T(8,128)(2,1)S(1)}, bf16[128,1024]{1,0:T(8,128)(2,1)}, u32[]{:S(2)}) copy-start(bf16[128,1024]{1,0:T(8,128)(2,1)} %param.6) | copy-start | bytes 786436
  104.4 9.6 %collective-permute-start.12 = (f32[128,1024]{1,0:T(8,128)S(1)}, f32[128,1024]{1,0:T(8,128)S(1)}, u32[]{:S(2)}, u32[]{:S(2)}) collective-permute-start(f32[128,1024]{1,0:T(8,128)S(1)} %fusion.17), channel_id=1, source_target_pairs={{0,4},{4,8},{8,12},{12,16},{16,20},{20,24},{24,28},{28,0},{1,5},{5... | collective-permute-start | bytes 1572872 | tf_op jit(solution)/shard_map/ppermute | solution.py:11
  114.4 9.6 %collective-permute-start.13 = (f32[128,1024]{1,0:T(8,128)S(1)}, f32[128,1024]{1,0:T(8,128)S(1)}, u32[]{:S(2)}, u32[]{:S(2)}) collective-permute-start(f32[128,1024]{1,0:T(8,128)S(1)} %convolution_add_fusion), channel_id=1, source_target_pairs={{0,4},{4,8},{8,12},{12,16},{16,20},{20,24},{24,28},{28,0},{1,5},{5... | collective-permute-start | bytes 1572872 | tf_op jit(solution)/shard_map/ppermute | solution.py:11
  124.3 9.6 %collective-permute-start.14 = (f32[128,1024]{1,0:T(8,128)S(1)}, f32[128,1024]{1,0:T(8,128)S(1)}, u32[]{:S(2)}, u32[]{:S(2)}) collective-permute-start(f32[128,1024]{1,0:T(8,128)S(1)} %fusion.21), channel_id=1, source_target_pairs={{0,4},{4,8},{8,12},{12,16},{16,20},{20,24},{24,28},{28,0},{1,5},{5... | collective-permute-start | bytes 1572872 | tf_op jit(solution)/shard_map/ppermute | solution.py:11
  133.8 10.7 %copy-start.1 = (bf16[128,1024]{1,0:T(8,128)(2,1)S(1)}, bf16[128,1024]{1,0:T(8,128)(2,1)}, u32[]{:S(2)}) copy-start(bf16[128,1024]{1,0:T(8,128)(2,1)} %param.7) | copy-start | bytes 786436
Sparse Core Ops, SparseCore 0:
  10.2 30.6 all-gather.5
  104.1 40.3 reduce-scatter.1
where the time goes:
time: 155 us
  waiting for transfers between devices  65.7 us (42%)
  blocking collectives  35.8 us (23%)
  starting transfers between devices  17.9 us (12%)
  between operations  14.9 us (10%)
  other arithmetic  10.8 us (7%)
  matrix products  8.74 us (6%)
    ppermute x15, waiting for transfers between devices, passed_along(): lax.ppermute(array, axis, [(i, (i + by) % count) for i in range(count)])  45.1 us
    all_gather x3, blocking collectives, combined_all(): gathered = jax.tree.map(lambda a: lax.all_gather(a, axis), part)  35.8 us
    ppermute x15, starting transfers between devices, passed_along(): lax.ppermute(array, axis, [(i, (i + by) % count) for i in range(count)])  17.8 us
    all_gather x1, waiting for transfers between devices, on_device(): home_tile = lax.all_gather(txt_own, 'rep', axis=0, tiled=True)  11.4 us
    reduce_scatter x1, waiting for transfers between devices, on_device(): lax.psum_scatter(text_terms, 'rep', scatter_dimension=0, tiled=True)  9.15 us
    dot_general x4, matrix products, tile_scores(): jnp.einsum('id,jd->ij', img_part, text_tile, preferred_element_type=jnp.f...  3.59 us
    dot_general x4, matrix products, on_device(): jnp.einsum('ij,id->jd', weight, tile, preferred_element_type=jnp.float32)  3.56 us
  transfers between devices with their start and end apart: 17, of which 10 were waited for; matrix products, arithmetic and copies ran while one was open for 7% of the time, Pallas kernels for 0%

commit v1 on v0

--- a/solution.py
+++ b/solution.py
@@ -55,7 +55,12 @@
     txt_unit, txt_inverse = normalize(text)
     img_tile = img_unit.astype(jnp.bfloat16)
     txt_own = txt_unit.astype(jnp.bfloat16)
-    home_tile = lax.all_gather(txt_own, "rep", axis=0, tiled=True)
+    ring = [txt_own]
+    for hop in range(3):
+        ring.append(lax.ppermute(ring[-1], "rep", [(dev, (dev + 1) % 4) for dev in range(4)]))
+    home_tile = jnp.roll(
+        jnp.concatenate(ring[::-1], axis=0), (lax.axis_index("rep") + 1) * ring[0].shape[0], axis=0
+    )
     block_rows = home_tile.shape[0]
     columns = lax.broadcasted_iota(jnp.int32, (row_count, block_rows), 1)
     onehot = (positive[0][:, None] == columns).astype(jnp.float32)

time: 155 us -> 155 us (level)
  local copies, waits for them, and re-layouts: 0.68 us -> 4.42 us
  starting transfers between devices: 17.9 us -> 14.3 us
  waiting for transfers between devices: 65.7 us -> 62.6 us
    ppermute x0 -> x3, waiting for transfers between devices: none -> 19.3 us  [on_device(): lax.ppermute(ring[-1], 'rep', [(dev, (dev + 1) % 4) for dev in range(4)])]
    all_gather x1 -> x0, waiting for transfers between devices: 11.4 us -> none  [on_device(): home_tile = lax.all_gather(txt_own, 'rep', axis=0, tiled=True)]
    ppermute x15, waiting for transfers between devices: 45.1 us -> 36.9 us  [passed_along(): lax.ppermute(array, axis, [(i, (i + by) % count) for i in range(count)])]
    ppermute x15, starting transfers between devices: 17.8 us -> 11.2 us  [passed_along(): lax.ppermute(array, axis, [(i, (i + by) % count) for i in range(count)])]
    unnamed x11 -> x33, local copies, waits for them, and re-layouts: 0.03 us -> 3.77 us
    ppermute x0 -> x3, starting transfers between devices: none -> 3.11 us  [on_device(): lax.ppermute(ring[-1], 'rep', [(dev, (dev + 1) % 4) for dev in range(4)])]
    reduce_scatter x1, waiting for transfers between devices: 9.15 us -> 6.36 us  [on_device(): lax.psum_scatter(text_terms, 'rep', scatter_dimension=0, tiled=True)]
    dot_general x4, matrix products: 1.59 us -> 3.39 us  [on_device(): jnp.dot(weight, home_tile, preferred_element_type=jnp.float32)]
  transfers between devices with their start and end apart: 17 -> 19, of which waited for: 10 -> 10; matrix products, arithmetic and copies ran while one was open for 7% -> 11% of each run, Pallas kernels for 0% -> 0%
where the time goes in v1:
time: 155 us; the launch traced here: 154 us
  waiting for transfers between devices  62.6 us (40%)
  blocking collectives  35.8 us (23%)
  between operations  15 us (10%)
  starting transfers between devices  14.3 us (9%)
  other arithmetic  11.5 us (7%)
  matrix products  10.2 us (7%)
  local copies, waits for them, and re-layouts  4.42 us (3%)
    ppermute x15, waiting for transfers between devices, passed_along(): lax.ppermute(array, axis, [(i, (i + by) % count) for i in range(count)])  36.9 us
    all_gather x3, blocking collectives, combined_all(): gathered = jax.tree.map(lambda a: lax.all_gather(a, axis), part)  35.8 us
    ppermute x3, waiting for transfers between devices, on_device(): lax.ppermute(ring[-1], 'rep', [(dev, (dev + 1) % 4) for dev in range(4)])  19.3 us
    ppermute x15, starting transfers between devices, passed_along(): lax.ppermute(array, axis, [(i, (i + by) % count) for i in range(count)])  11.2 us
    reduce_scatter x1, waiting for transfers between devices, on_device(): lax.psum_scatter(text_terms, 'rep', scatter_dimension=0, tiled=True)  6.36 us
    dot_general x4, matrix products, on_device(): jnp.einsum('ij,id->jd', weight, tile, preferred_element_type=jnp.float32)  4.56 us
    unnamed x33, local copies, waits for them, and re-layouts  3.77 us
    dot_general x4, matrix products, on_device(): jnp.dot(weight, home_tile, preferred_element_type=jnp.float32)  3.39 us
  transfers between devices with their start and end apart: 19, of which 10 were waited for; matrix products, arithmetic and copies ran while one was open for 11% of the time, Pallas kernels for 0%

profile of v1, /device:TPU:0, one launch (start us, length us, event | category | flops | bytes accessed | tf_op | source)
XLA Modules:
  0.0 154.0 jit_solution(2970192780338975937)
XLA Ops:
  7.2 1.1 fusion.13
  8.3 1.1 fusion.2
  9.4 3.1 %collective-permute-start = (bf16[128,1024]{1,0:T(8,128)(2,1)S(1)}, bf16[128,1024]{1,0:T(8,128)(2,1)S(1)}, u32[]{:S(2)}, u32[]{:S(2)}) collective-permute-start(bf16[128,1024]{1,0:T(8,128)(2,1)S(1)} %fusion.2), channel_id=1, source_target_pairs={{0,1},{1,2},{2,3},{3,0},{4,5},{5,6},{6,7},{7,4},{8,9},{9,10},{10,1... | collective-permute-start | bytes 786440 | tf_op jit(solution)/shard_map/ppermute | solution.py:60
  12.5 1.1 fusion.9
  13.6 1.1 fusion.5
  14.7 1.7 %collective-permute-start.4 = (bf16[128,1024]{1,0:T(8,128)(2,1)S(1)}, bf16[128,1024]{1,0:T(8,128)(2,1)S(1)}, u32[]{:S(2)}, u32[]{:S(2)}) collective-permute-start(bf16[128,1024]{1,0:T(8,128)(2,1)S(1)} %fusion.5), channel_id=1, source_target_pairs={{0,28},{4,0},{8,4},{12,8},{16,12},{20,16},{24,20},{28,24},{1,29},{... | collective-permute-start | bytes 786440 | tf_op jit(solution)/shard_map/ppermute | solution.py:11
  16.4 4.5 %collective-permute-done = bf16[128,1024]{1,0:T(8,128)(2,1)S(1)} collective-permute-done((bf16[128,1024]{1,0:T(8,128)(2,1)S(1)}, bf16[128,1024]{1,0:T(8,128)(2,1)S(1)}, u32[]{:S(2)}, u32[]{:S(2)}) %collective-permute-start) | collective-permute-done | bytes 262176 | tf_op jit(solution)/shard_map/ppermute | solution.py:60
  20.9 2.2 %collective-permute-start.6 = (bf16[128,1024]{1,0:T(8,128)(2,1)S(1)}, bf16[128,1024]{1,0:T(8,128)(2,1)S(1)}, u32[]{:S(2)}, u32[]{:S(2)}) collective-permute-start(bf16[128,1024]{1,0:T(8,128)(2,1)S(1)} %collective-permute-done.4), channel_id=1, source_target_pairs={{0,28},{4,0},{8,4},{12,8},{16,12},{20,16},{24,20},{28,24},{1,29},{... | collective-permute-start | bytes 786440 | tf_op jit(solution)/shard_map/ppermute | solution.py:11
  23.1 7.1 %collective-permute-done.1 = bf16[128,1024]{1,0:T(8,128)(2,1)S(1)} collective-permute-done((bf16[128,1024]{1,0:T(8,128)(2,1)S(1)}, bf16[128,1024]{1,0:T(8,128)(2,1)S(1)}, u32[]{:S(2)}, u32[]{:S(2)}) %collective-permute-start.1) | collective-permute-done | bytes 262176 | tf_op jit(solution)/shard_map/ppermute | solution.py:60
  30.9 7.8 %collective-permute-done.2 = bf16[128,1024]{1,0:T(8,128)(2,1)} collective-permute-done((bf16[128,1024]{1,0:T(8,128)(2,1)S(1)}, bf16[128,1024]{1,0:T(8,128)(2,1)}, u32[]{:S(2)}, u32[]{:S(2)}) %collective-permute-start.2) | collective-permute-done | bytes 262176 | tf_op jit(solution)/shard_map/ppermute | solution.py:60
  38.6 1.0 constant_dynamic-update-slice_fusion.7
  42.8 11.9 %all-gather.3 = f32[4,1,512]{2,1,0:T(1,128)S(1)} all-gather(f32[1,1,512]{2,1,0:T(1,128)S(1)} %bitcast.69), channel_id=2, replica_groups=mesh['blk'=8,'rep'=4] {'rep'}, dimensions={0}, use_global_device_ids=true | all-gather | bytes 10240 | tf_op jit(solution)/shard_map/all_gather | solution.py:15
  54.8 2.1 %collective-permute-start.9 = (f32[128]{0:T(128)S(1)}, f32[128]{0:T(128)S(1)}, u32[]{:S(2)}, u32[]{:S(2)}) collective-permute-start(f32[128]{0:T(128)S(1)} %get-tuple-element.188), channel_id=1, source_target_pairs={{0,28},{4,0},{8,4},{12,8},{16,12},{20,16},{24,20},{28,24},{1,29},{... | collective-permute-start | bytes 1544 | tf_op jit(solution)/shard_map/ppermute | solution.py:11
  59.7 1.1 collective-permute-start.10
  60.8 2.6 %collective-permute-start.7 = (f32[128]{0:T(128)S(1)}, f32[128]{0:T(128)S(1)}, u32[]{:S(2)}, u32[]{:S(2)}) collective-permute-start(f32[128]{0:T(128)S(1)} %max.62), channel_id=1, source_target_pairs={{0,28},{4,0},{8,4},{12,8},{16,12},{20,16},{24,20},{28,24},{1,29},{... | collective-permute-start | bytes 1544 | tf_op jit(solution)/shard_map/ppermute | solution.py:11
  63.6 1.1 collective-permute-start.11
  64.9 11.9 %all-gather.2 = f32[4,1,512]{2,1,0:T(1,128)S(1)} all-gather(f32[1,1,512]{2,1,0:T(1,128)S(1)} %get-tuple-element.223), channel_id=1, replica_groups=mesh['blk'=8,'rep'=4] {'rep'}, dimensions={0}, use_global_device_ids=true | all-gather | bytes 10240 | tf_op jit(solution)/shard_map/all_gather | solution.py:15
  76.9 11.9 %all-gather.1 = f32[4,1,512]{2,1,0:T(1,128)S(1)} all-gather(f32[1,1,512]{2,1,0:T(1,128)S(1)} %get-tuple-element.224), channel_id=1, replica_groups=mesh['blk'=8,'rep'=4] {'rep'}, dimensions={0}, use_global_device_ids=true | all-gather | bytes 10240 | tf_op jit(solution)/shard_map/all_gather | solution.py:15
  89.2 3.9 %collective-permute-done.12 = f32[128]{0:T(128)S(1)} collective-permute-done((f32[128]{0:T(128)S(1)}, f32[128]{0:T(128)S(1)}, u32[]{:S(2)}, u32[]{:S(2)}) %collective-permute-start.12) | collective-permute-done | bytes 544 | tf_op jit(solution)/shard_map/ppermute | solution.py:11
  93.1 1.5 fusion.40
  94.6 2.3 %collective-permute-done.13 = f32[128]{0:T(128)S(1)} collective-permute-done((f32[128]{0:T(128)S(1)}, f32[128]{0:T(128)S(1)}, u32[]{:S(2)}, u32[]{:S(2)}) %collective-permute-start.13) | collective-permute-done | bytes 544 | tf_op jit(solution)/shard_map/ppermute | solution.py:11
  97.5 3.3 %collective-permute-done.14 = f32[128]{0:T(128)S(1)} collective-permute-done((f32[128]{0:T(128)S(1)}, f32[128]{0:T(128)S(1)}, u32[]{:S(2)}, u32[]{:S(2)}) %collective-permute-start.14) | collective-permute-done | bytes 544 | tf_op jit(solution)/shard_map/ppermute | solution.py:11
  101.4 1.9 %add_add_fusion = f32[512,1024]{1,0:T(8,128)} fusion(f32[512,1024]{1,0:T(8,128)S(1)} %fusion.42, f32[512,1024]{1,0:T(8,128)S(1)} %fusion.41, f32[512,1024]{1,0:T(8,128)S(1)} %fusion.40, bf16[128,1024]{1,0:T(8,128)(2,1)S(1)} %copy-done.8, f32[128,512]{1,0:T(8,128)S(1)} %get-tuple-element.228, f32[512]{0:T(512)S(1)} %get-tuple-element.220, ...), kind=kOutput, calls=%fused_computation.4 | convolution fusion | flops 136118272 | bytes 8915456 | tf_op jit(solution)/shard_map/ij,id->jd/dot_general | solution.py:108
  104.2 9.1 %collective-permute-done.15 = f32[128,1024]{1,0:T(8,128)S(1)} collective-permute-done((f32[128,1024]{1,0:T(8,128)S(1)}, f32[128,1024]{1,0:T(8,128)S(1)}, u32[]{:S(2)}, u32[]{:S(2)}) %collective-permute-start.15) | collective-permute-done | bytes 524320 | tf_op jit(solution)/shard_map/ppermute | solution.py:11
  113.4 9.5 %collective-permute-done.16 = f32[128,1024]{1,0:T(8,128)S(1)} collective-permute-done((f32[128,1024]{1,0:T(8,128)S(1)}, f32[128,1024]{1,0:T(8,128)S(1)}, u32[]{:S(2)}, u32[]{:S(2)}) %collective-permute-start.16) | collective-permute-done | bytes 524320 | tf_op jit(solution)/shard_map/ppermute | solution.py:11
  122.9 1.2 fusion.29
  125.2 8.7 %collective-permute-done.17 = f32[128,1024]{1,0:T(8,128)} collective-permute-done((f32[128,1024]{1,0:T(8,128)}, f32[128,1024]{1,0:T(8,128)}, u32[]{:S(2)}, u32[]{:S(2)}) %collective-permute-start.17) | collective-permute-done | bytes 524320 | tf_op jit(solution)/shard_map/ppermute | solution.py:11
  133.9 1.5 fusion.6
  135.4 2.1 %fusion.8 = f32[128,1024]{1,0:T(8,128)} fusion(bf16[128,1024]{1,0:T(8,128)(2,1)S(1)} %copy-done.1, f32[128]{0:T(128)S(1)} %get-tuple-element.229, f32[128]{0:T(128)S(1)} %add_rsqrt_fusion.1, f32[128,1024]{1,0:T(8,128)} %collective-permute-done.17, f32[128,1024]{1,0:T(8,128)S(1)} %get-tuple-element.230, f32[]{:T(128)} %bitcast.48), kind=kLoop, calls=%fused_computation.21 | loop fusion | flops 917504 | bytes 1836036 | tf_op jit(solution)/shard_map/mul | solution.py:117
  137.5 6.4 %reduce-scatter.2.cloned.1.call-done = f32[128,1024]{1,0:T(8,128)} async-done(((f32[512,1024]{1,0:T(8,128)}), f32[128,1024]{1,0:T(8,128)}) %reduce-scatter.2.cloned.1.call-update) | async-done | bytes 524304 | tf_op jit(solution)/shard_map/reduce_scatter | solution.py:114
  143.8 1.3 fusion.10
  145.1 2.1 %fusion.12 = f32[128,1024]{1,0:T(8,128)} fusion(bf16[128,1024]{1,0:T(8,128)(2,1)S(1)} %copy-done, f32[128,1024]{1,0:T(8,128)} %reduce-scatter.2.cloned.1.call-done, f32[128]{0:T(128)S(1)} %fusion.10, f32[]{:T(128)} %bitcast.46, f32[128]{0:T(128)S(1)} %add_rsqrt_fusion), kind=kLoop, calls=%fused_computation.25 | loop fusion | flops 786432 | bytes 1311748 | tf_op jit(solution)/shard_map/mul | solution.py:120
  (97 shorter events, 10.1 us)
Async XLA Ops:
  7.2 33.5 %copy-start = (bf16[128,1024]{1,0:T(8,128)(2,1)S(1)}, bf16[128,1024]{1,0:T(8,128)(2,1)}, u32[]{:S(2)}) copy-start(bf16[128,1024]{1,0:T(8,128)(2,1)} %param.7) | copy-start | bytes 786436
  7.2 136.7 %reduce-scatter.2.cloned.1.call-start = ((), (), s32[]{:S(2)}) async-start(), calls=%async_computation.1 | async-start | bytes 2621440 | tf_op jit(solution)/shard_map/reduce_scatter | solution.py:114
  9.4 11.4 %collective-permute-start = (bf16[128,1024]{1,0:T(8,128)(2,1)S(1)}, bf16[128,1024]{1,0:T(8,128)(2,1)S(1)}, u32[]{:S(2)}, u32[]{:S(2)}) collective-permute-start(bf16[128,1024]{1,0:T(8,128)(2,1)S(1)} %fusion.2), channel_id=1, source_target_pairs={{0,1},{1,2},{2,3},{3,0},{4,5},{5,6},{6,7},{7,4},{8,9},{9,10},{10,1... | collective-permute-start | bytes 786440 | tf_op jit(solution)/shard_map/ppermute | solution.py:60
  14.7 27.3 %copy-start.2 = (bf16[128,1024]{1,0:T(8,128)(2,1)}, bf16[128,1024]{1,0:T(8,128)(2,1)S(1)}, u32[]{:S(2)}) copy-start(bf16[128,1024]{1,0:T(8,128)(2,1)S(1)} %fusion.5) | copy-start | bytes 786436
  14.7 6.2 %collective-permute-start.4 = (bf16[128,1024]{1,0:T(8,128)(2,1)S(1)}, bf16[128,1024]{1,0:T(8,128)(2,1)S(1)}, u32[]{:S(2)}, u32[]{:S(2)}) collective-permute-start(bf16[128,1024]{1,0:T(8,128)(2,1)S(1)} %fusion.5), channel_id=1, source_target_pairs={{0,28},{4,0},{8,4},{12,8},{16,12},{20,16},{24,20},{28,24},{1,29},{... | collective-permute-start | bytes 786440 | tf_op jit(solution)/shard_map/ppermute | solution.py:11
  20.9 9.3 %collective-permute-start.1 = (bf16[128,1024]{1,0:T(8,128)(2,1)S(1)}, bf16[128,1024]{1,0:T(8,128)(2,1)S(1)}, u32[]{:S(2)}, u32[]{:S(2)}) collective-permute-start(bf16[128,1024]{1,0:T(8,128)(2,1)S(1)} %collective-permute-done), channel_id=1, source_target_pairs={{0,1},{1,2},{2,3},{3,0},{4,5},{5,6},{6,7},{7,4},{8,9},{9,10},{10,1... | collective-permute-start | bytes 786440 | tf_op jit(solution)/shard_map/ppermute | solution.py:60
  20.9 36.0 %copy-start.4 = (bf16[128,1024]{1,0:T(8,128)(2,1)}, bf16[128,1024]{1,0:T(8,128)(2,1)S(1)}, u32[]{:S(2)}) copy-start(bf16[128,1024]{1,0:T(8,128)(2,1)S(1)} %collective-permute-done.4) | copy-start | bytes 786436
  20.9 9.9 %collective-permute-start.6 = (bf16[128,1024]{1,0:T(8,128)(2,1)S(1)}, bf16[128,1024]{1,0:T(8,128)(2,1)S(1)}, u32[]{:S(2)}, u32[]{:S(2)}) collective-permute-start(bf16[128,1024]{1,0:T(8,128)(2,1)S(1)} %collective-permute-done.4), channel_id=1, source_target_pairs={{0,28},{4,0},{8,4},{12,8},{16,12},{20,16},{24,20},{28,24},{1,29},{... | collective-permute-start | bytes 786440 | tf_op jit(solution)/shard_map/ppermute | solution.py:11
  30.1 0.8 copy-start.9
  30.1 8.5 %collective-permute-start.2 = (bf16[128,1024]{1,0:T(8,128)(2,1)S(1)}, bf16[128,1024]{1,0:T(8,128)(2,1)}, u32[]{:S(2)}, u32[]{:S(2)}) collective-permute-start(bf16[128,1024]{1,0:T(8,128)(2,1)S(1)} %collective-permute-done.1), channel_id=1, source_target_pairs={{0,1},{1,2},{2,3},{3,0},{4,5},{5,6},{6,7},{7,4},{8,9},{9,10},{10,1... | collective-permute-start | bytes 786440 | tf_op jit(solution)/shard_map/ppermute | solution.py:60
  30.8 26.7 %copy-start.6 = (bf16[128,1024]{1,0:T(8,128)(2,1)}, bf16[128,1024]{1,0:T(8,128)(2,1)S(1)}, u32[]{:S(2)}) copy-start(bf16[128,1024]{1,0:T(8,128)(2,1)S(1)} %collective-permute-done.6) | copy-start | bytes 786436
  30.8 27.2 %collective-permute-start.8 = (bf16[128,1024]{1,0:T(8,128)(2,1)S(1)}, bf16[128,1024]{1,0:T(8,128)(2,1)S(1)}, u32[]{:S(2)}, u32[]{:S(2)}) collective-permute-start(bf16[128,1024]{1,0:T(8,128)(2,1)S(1)} %collective-permute-done.6), channel_id=1, source_target_pairs={{0,28},{4,0},{8,4},{12,8},{16,12},{20,16},{24,20},{28,24},{1,29},{... | collective-permute-start | bytes 786440 | tf_op jit(solution)/shard_map/ppermute | solution.py:11
  38.6 3.1 %copy-start.10 = (bf16[128,1024]{1,0:T(8,128)(2,1)S(1)}, bf16[128,1024]{1,0:T(8,128)(2,1)}, u32[]{:S(2)}) copy-start(bf16[128,1024]{1,0:T(8,128)(2,1)} %copy-done.9) | copy-start | bytes 786436
  40.7 1.9 %copy-start.11 = (s32[1,128]{1,0:T(1,128)S(1)}, s32[1,128]{1,0:T(1,128)}, u32[]{:S(2)}) copy-start(s32[1,128]{1,0:T(1,128)} %param.8) | copy-start | bytes 1540
  54.7 4.6 %collective-permute-start.3 = (f32[128]{0:T(128)S(1)}, f32[128]{0:T(128)S(1)}, u32[]{:S(2)}, u32[]{:S(2)}) collective-permute-start(f32[128]{0:T(128)S(1)} %get-tuple-element.198), channel_id=1, source_target_pairs={{0,28},{4,0},{8,4},{12,8},{16,12},{20,16},{24,20},{28,24},{1,29},{... | collective-permute-start | bytes 1544 | tf_op jit(solution)/shard_map/ppermute | solution.py:11
  54.8 4.9 %collective-permute-start.9 = (f32[128]{0:T(128)S(1)}, f32[128]{0:T(128)S(1)}, u32[]{:S(2)}, u32[]{:S(2)}) collective-permute-start(f32[128]{0:T(128)S(1)} %get-tuple-element.188), channel_id=1, source_target_pairs={{0,28},{4,0},{8,4},{12,8},{16,12},{20,16},{24,20},{28,24},{1,29},{... | collective-permute-start | bytes 1544 | tf_op jit(solution)/shard_map/ppermute | solution.py:11
  58.0 0.7 copy-start.7
  59.3 1.4 collective-permute-start.5
  59.7 3.9 %collective-permute-start.10 = (f32[128]{0:T(128)S(1)}, f32[128]{0:T(128)S(1)}, u32[]{:S(2)}, u32[]{:S(2)}) collective-permute-start(f32[128]{0:T(128)S(1)} %multiply_add_fusion.2), channel_id=1, source_target_pairs={{0,28},{4,0},{8,4},{12,8},{16,12},{20,16},{24,20},{28,24},{1,29},{... | collective-permute-start | bytes 1544 | tf_op jit(solution)/shard_map/ppermute | solution.py:11
  60.8 3.9 %collective-permute-start.7 = (f32[128]{0:T(128)S(1)}, f32[128]{0:T(128)S(1)}, u32[]{:S(2)}, u32[]{:S(2)}) collective-permute-start(f32[128]{0:T(128)S(1)} %max.62), channel_id=1, source_target_pairs={{0,28},{4,0},{8,4},{12,8},{16,12},{20,16},{24,20},{28,24},{1,29},{... | collective-permute-start | bytes 1544 | tf_op jit(solution)/shard_map/ppermute | solution.py:11
  63.6 25.5 %collective-permute-start.11 = (f32[128]{0:T(128)S(1)}, f32[128]{0:T(128)S(1)}, u32[]{:S(2)}, u32[]{:S(2)}) collective-permute-start(f32[128]{0:T(128)S(1)} %multiply_add_fusion.1), channel_id=1, source_target_pairs={{0,28},{4,0},{8,4},{12,8},{16,12},{20,16},{24,20},{28,24},{1,29},{... | collective-permute-start | bytes 1544 | tf_op jit(solution)/shard_map/ppermute | solution.py:11
  89.1 7.9 %copy-start.5 = (bf16[128,1024]{1,0:T(8,128)(2,1)S(1)}, bf16[128,1024]{1,0:T(8,128)(2,1)}, u32[]{:S(2)}) copy-start(bf16[128,1024]{1,0:T(8,128)(2,1)} %copy-done.4) | copy-start | bytes 786436
  89.1 3.9 %collective-permute-start.12 = (f32[128]{0:T(128)S(1)}, f32[128]{0:T(128)S(1)}, u32[]{:S(2)}, u32[]{:S(2)}) collective-permute-start(f32[128]{0:T(128)S(1)} %log_add_fusion.1), channel_id=1, source_target_pairs={{0,4},{4,8},{8,12},{12,16},{16,20},{20,24},{24,28},{28,0},{1,5},{5... | collective-permute-start | bytes 1544 | tf_op jit(solution)/shard_map/ppermute | solution.py:11
  93.1 3.9 %collective-permute-start.13 = (f32[128]{0:T(128)S(1)}, f32[128]{0:T(128)S(1)}, u32[]{:S(2)}, u32[]{:S(2)}) collective-permute-start(f32[128]{0:T(128)S(1)} %collective-permute-done.12), channel_id=1, source_target_pairs={{0,4},{4,8},{8,12},{12,16},{16,20},{20,24},{24,28},{28,0},{1,5},{5... | collective-permute-start | bytes 1544 | tf_op jit(solution)/shard_map/ppermute | solution.py:11
  93.1 7.8 %copy-start.3 = (bf16[128,1024]{1,0:T(8,128)(2,1)S(1)}, bf16[128,1024]{1,0:T(8,128)(2,1)}, u32[]{:S(2)}) copy-start(bf16[128,1024]{1,0:T(8,128)(2,1)} %copy-done.2) | copy-start | bytes 786436
  94.6 6.8 %copy-start.8 = (bf16[128,1024]{1,0:T(8,128)(2,1)S(1)}, bf16[128,1024]{1,0:T(8,128)(2,1)}, u32[]{:S(2)}) copy-start(bf16[128,1024]{1,0:T(8,128)(2,1)} %copy-done.7) | copy-start | bytes 786436
  96.9 3.9 %collective-permute-start.14 = (f32[128]{0:T(128)S(1)}, f32[128]{0:T(128)S(1)}, u32[]{:S(2)}, u32[]{:S(2)}) collective-permute-start(f32[128]{0:T(128)S(1)} %collective-permute-done.13), channel_id=1, source_target_pairs={{0,4},{4,8},{8,12},{12,16},{16,20},{20,24},{24,28},{28,0},{1,5},{5... | collective-permute-start | bytes 1544 | tf_op jit(solution)/shard_map/ppermute | solution.py:11
  103.7 9.6 %collective-permute-start.15 = (f32[128,1024]{1,0:T(8,128)S(1)}, f32[128,1024]{1,0:T(8,128)S(1)}, u32[]{:S(2)}, u32[]{:S(2)}) collective-permute-start(f32[128,1024]{1,0:T(8,128)S(1)} %fusion.23), channel_id=1, source_target_pairs={{0,4},{4,8},{8,12},{12,16},{16,20},{20,24},{24,28},{28,0},{1,5},{5... | collective-permute-start | bytes 1572872 | tf_op jit(solution)/shard_map/ppermute | solution.py:11
  104.2 29.7 %copy-start.1 = (bf16[128,1024]{1,0:T(8,128)(2,1)S(1)}, bf16[128,1024]{1,0:T(8,128)(2,1)}, u32[]{:S(2)}) copy-start(bf16[128,1024]{1,0:T(8,128)(2,1)} %param.6) | copy-start | bytes 786436
  113.4 9.6 %collective-permute-start.16 = (f32[128,1024]{1,0:T(8,128)S(1)}, f32[128,1024]{1,0:T(8,128)S(1)}, u32[]{:S(2)}, u32[]{:S(2)}) collective-permute-start(f32[128,1024]{1,0:T(8,128)S(1)} %add.184), channel_id=1, source_target_pairs={{0,4},{4,8},{8,12},{12,16},{16,20},{20,24},{24,28},{28,0},{1,5},{5... | collective-permute-start | bytes 1572872 | tf_op jit(solution)/shard_map/ppermute | solution.py:11
  124.1 9.8 %collective-permute-start.17 = (f32[128,1024]{1,0:T(8,128)}, f32[128,1024]{1,0:T(8,128)}, u32[]{:S(2)}, u32[]{:S(2)}) collective-permute-start(f32[128,1024]{1,0:T(8,128)} %fusion.29), channel_id=1, source_target_pairs={{0,4},{4,8},{8,12},{12,16},{16,20},{20,24},{24,28},{28,0},{1,5},{5... | collective-permute-start | bytes 1572872 | tf_op jit(solution)/shard_map/ppermute | solution.py:11
Sparse Core Ops, SparseCore 0:
  103.5 40.3 reduce-scatter.1
